TPU v7x, 32 devices: a whole 2x2x4 slice. The times are simulated.
32 devices in a mesh: gx: 2 (over y), gy: 4 (over x, core), gz: 4 (over z).
Axes of the slice: x: 2, y: 2, z: 4, core: 2. Of those that a mesh axis runs over, the one named last changes fastest.
Arguments:
- pressure: float32 [24, 64, 512], P('gx', 'gy', 'gz'), may hold values from -8 to 8
- wind: float32 [3, 24, 64, 512], P(None, 'gx', 'gy', 'gz'), may hold values from -6 to 6
Outputs:
- result: float32 [24, 64, 512], P('gx', 'gy', 'gz')
All inputs are finite; a program needn't handle non-finite values.
Results may differ from a plain program's by a relative error of at most 0.00019.
Values sent between devices are 32-bit elements; how exact they have to be, the bound alone decides.
A program may use at most 64 MiB of HBM per device.

v0:
```python
import jax
import jax.numpy as jnp
from jax import lax
from jax.sharding import PartitionSpec as P

SWEEPS = 2
COARSE_SWEEPS = 4


OMEGA = 0.8
VISCOSITY = 1.0
REACTION = 1.0


def with_halo(cells, sides, width):
    for axis, dim in sides:
        count = lax.axis_size(axis)
        ends = count - 1
        head = lax.slice_in_dim(cells, 0, width, axis=dim)
        tail = lax.slice_in_dim(cells, cells.shape[dim] - width, cells.shape[dim], axis=dim)
        cells = jnp.concatenate(
            [
                lax.ppermute(tail, axis, [(i, (i + 1) % count) for i in range(ends)]),
                cells,
                lax.ppermute(head, axis, [((i + 1) % count, i) for i in range(ends)]),
            ],
            axis=dim,
        )
    return cells


def six_sum(padded):
    return (
        padded[..., 2:, 1:-1, 1:-1]
        + padded[..., :-2, 1:-1, 1:-1]
        + padded[..., 1:-1, 2:, 1:-1]
        + padded[..., 1:-1, :-2, 1:-1]
        + padded[..., 1:-1, 1:-1, 2:]
        + padded[..., 1:-1, 1:-1, :-2]
    )


def central_parts(padded):
    return (
        (padded[..., 2:, 1:-1, 1:-1] - padded[..., :-2, 1:-1, 1:-1]) * 0.5,
        (padded[..., 1:-1, 2:, 1:-1] - padded[..., 1:-1, :-2, 1:-1]) * 0.5,
        (padded[..., 1:-1, 1:-1, 2:] - padded[..., 1:-1, 1:-1, :-2]) * 0.5,
    )


def crop(values, margin):
    return values[..., margin:-margin, margin:-margin, margin:-margin]


def axis_inside(position, extent, pieces, rim_width):
    places = position * extent + jnp.arange(-rim_width, extent + rim_width, dtype=jnp.int32)
    return ((places >= 0) & (places < extent * pieces)).astype(jnp.float32)


def inside_mask(extents, rim_width):
    along_x = axis_inside(lax.axis_index("gx"), extents[0], lax.axis_size("gx"), rim_width)
    along_y = axis_inside(lax.axis_index("gy"), extents[1], lax.axis_size("gy"), rim_width)
    along_z = axis_inside(lax.axis_index("gz"), extents[2], lax.axis_size("gz"), rim_width)
    return along_x[:, None, None] * along_y[None, :, None] * along_z[None, None, :]


def laplace(values, padded, weight_scale):
    return weight_scale * (6.0 * values - six_sum(padded))


def sweep(source, values, padded, weight_scale):
    return values + OMEGA / (6.0 * weight_scale) * (source - laplace(values, padded, weight_scale))


def start_sweep(source, weight_scale):
    return OMEGA / (6.0 * weight_scale) * source


def smooth_faces(values):
    return with_halo(values, (("gx", 0), ("gy", 1), ("gz", 2)), 1)


def smooth(source, values, weight_scale, sweep_count):
    for sweep_number in range(sweep_count):
        if values is None:
            values = start_sweep(source, weight_scale)
        else:
            values = sweep(source, values, smooth_faces(values), weight_scale)
    return values


def coarse_solve(source, weight_scale):
    reach = COARSE_SWEEPS - 1
    padded_source = with_halo(source, (("gx", 0), ("gy", 1), ("gz", 2)), reach)
    values = start_sweep(padded_source, weight_scale)
    for sweep_number in range(1, COARSE_SWEEPS):
        rim_width = reach - sweep_number
        values = sweep(crop(padded_source, sweep_number), crop(values, 1), values, weight_scale)
        if rim_width > 0:
            values = values * inside_mask(source.shape, rim_width)
    return values


def restrict(values):
    extent_x, extent_y, extent_z = values.shape
    blocks = values.reshape(extent_x // 2, 2, extent_y // 2, 2, extent_z // 2, 2)
    return 0.125 * jnp.sum(blocks, axis=(1, 3, 5))


def prolong(values):
    extent_x, extent_y, extent_z = values.shape
    spread = jnp.broadcast_to(
        values[:, None, :, None, :, None], (extent_x, 2, extent_y, 2, extent_z, 2)
    )
    return spread.reshape(2 * extent_x, 2 * extent_y, 2 * extent_z)


def vcycle(source, values, depth_index):
    weight_scale = 0.25**depth_index
    if depth_index == 2:
        return coarse_solve(source, weight_scale)
    values = smooth(source, values, weight_scale, SWEEPS)
    residual = source - laplace(values, smooth_faces(values), weight_scale)
    correction = vcycle(restrict(residual), None, depth_index + 1)
    values = values + prolong(correction)
    return smooth(source, values, weight_scale, SWEEPS)


def solve(source):
    values = None
    values = vcycle(source, values, 0)
    return values


def momentum(padded_velocity, wind):
    centre = padded_velocity[:, 1:-1, 1:-1, 1:-1]
    diffusion = 6.0 * centre - six_sum(padded_velocity)
    slopes = central_parts(padded_velocity)
    convection = wind[0:1] * slopes[0] + wind[1:2] * slopes[1] + wind[2:3] * slopes[2]
    return REACTION * centre + VISCOSITY * diffusion + convection


def body(pressure, wind):
    first = solve(pressure)
    padded = with_halo(first, (("gx", 0), ("gy", 1), ("gz", 2)), 1)
    velocity = jnp.stack(central_parts(padded))
    padded_velocity = with_halo(velocity, (("gx", 1), ("gy", 2), ("gz", 3)), 1)
    flux = momentum(padded_velocity, wind)
    padded_flux = with_halo(flux, (("gx", 1), ("gy", 2), ("gz", 3)), 1)
    slopes = central_parts(padded_flux)
    product = -(slopes[0][0] + slopes[1][1] + slopes[2][2])
    return solve(product)


def solution(mesh):
    in_specs = (P("gx", "gy", "gz"), P(None, "gx", "gy", "gz"))
    out_specs = P("gx", "gy", "gz")
    return jax.shard_map(body, mesh=mesh, in_specs=in_specs, out_specs=out_specs, check_vma=False)
```

profile of v0, /device:TPU:0, one launch (start us, length us, event | category | flops | bytes accessed | tf_op | source)
XLA Modules:
  0.0 551.5 jit_solution(5317152724919394749)
XLA Ops:
  2.2 4.9 collective-permute-start.1
  15.1 5.2 collective-permute-start.5
  39.7 5.0 collective-permute-start.11
  49.9 7.7 %reshape.155 = f32[6,2,8,2,64,2]{5,4,3,2,1,0:T(8,128)} reshape(f32[12,16,128]{2,1,0:T(8,128)S(1)} %fusion.97) | data formatting | bytes 196608 | tf_op jit(solution)/shard_map/reshape | solution.py:106
  74.6 5.0 collective-permute-start.17
  95.3 5.0 collective-permute-start.23
  117.8 5.8 %collective-permute-done.27 = f32[9,3,32]{2,1,0:T(4,128)S(1)} collective-permute-done((f32[9,3,32]{2,1,0:T(4,128)S(1)}, f32[9,3,32]{2,1,0:T(4,128)S(1)}, u32[]{:S(2)}, u32[]{:S(2)}) %collective-permute-start.27) | collective-permute-done | bytes 3488 | tf_op jit(solution)/shard_map/ppermute | solution.py:25
  169.3 4.9 collective-permute-start.41
  179.8 5.6 %reshape.158 = f32[12,16,128]{2,1,0:T(8,128)S(1)} reshape(f32[6,2,8,2,64,2]{5,4,3,2,1,0:T(8,128)} %broadcast_in_dim.9) | data formatting | bytes 196608 | tf_op jit(solution)/shard_map/reshape | solution.py:115
  216.8 5.1 collective-permute-start.51
  240.4 5.1 collective-permute-start.57
  264.3 5.1 collective-permute-start.63
  271.8 4.9 collective-permute-start.65
  276.8 6.5 %collective-permute-done.64 = f32[3,14,18,1]{3,2,1,0:T(8,128)S(1)} collective-permute-done((f32[3,14,18,1]{3,2,1,0:T(8,128)S(1)}, f32[3,14,18,1]{3,2,1,0:T(8,128)S(1)}, u32[]{:S(2)}, u32[]{:S(2)}) %collective-permute-start.64) | collective-permute-done | bytes 3056 | tf_op jit(solution)/shard_map/ppermute | solution.py:25
  294.1 5.2 collective-permute-start.69
  306.5 5.5 collective-permute-done.70
  322.4 6.4 %collective-permute-start.75 = (f32[14,1,128]{2,1,0:T(1,128)S(1)}, f32[14,1,128]{2,1,0:T(1,128)S(1)}, u32[]{:S(2)}, u32[]{:S(2)}) collective-permute-start(f32[14,1,128]{2,1,0:T(1,128)S(1)} %get-tuple-element.50), channel_id=1, source_target_pairs={{0,4},{4,8},{8,12},{1,5},{5,9},{9,13},{2,6},{6,10},{10,14},{3,7},{... | collective-permute-start | bytes 21512 | tf_op jit(solution)/shard_map/ppermute | solution.py:23
  347.4 7.4 %collective-permute-start.81 = (f32[14,1,128]{2,1,0:T(1,128)S(1)}, f32[14,1,128]{2,1,0:T(1,128)S(1)}, u32[]{:S(2)}, u32[]{:S(2)}) collective-permute-start(f32[14,1,128]{2,1,0:T(1,128)S(1)} %get-tuple-element.48), channel_id=1, source_target_pairs={{0,4},{4,8},{8,12},{1,5},{5,9},{9,13},{2,6},{6,10},{10,14},{3,7},{... | collective-permute-start | bytes 21512 | tf_op jit(solution)/shard_map/ppermute | solution.py:23
  365.0 7.7 %reshape.159 = f32[6,2,8,2,64,2]{5,4,3,2,1,0:T(8,128)} reshape(f32[12,16,128]{2,1,0:T(8,128)S(1)} %fusion.49) | data formatting | bytes 196608 | tf_op jit(solution)/shard_map/reshape | solution.py:106
  384.5 4.9 collective-permute-start.87
  406.9 5.0 collective-permute-start.93
  436.9 5.8 %collective-permute-done.99 = f32[9,3,32]{2,1,0:T(4,128)S(1)} collective-permute-done((f32[9,3,32]{2,1,0:T(4,128)S(1)}, f32[9,3,32]{2,1,0:T(4,128)S(1)}, u32[]{:S(2)}, u32[]{:S(2)}) %collective-permute-start.99) | collective-permute-done | bytes 3488 | tf_op jit(solution)/shard_map/ppermute | solution.py:25
  498.9 5.6 %reshape.162 = f32[12,16,128]{2,1,0:T(8,128)S(1)} reshape(f32[6,2,8,2,64,2]{5,4,3,2,1,0:T(8,128)} %broadcast_in_dim.11) | data formatting | bytes 196608 | tf_op jit(solution)/shard_map/reshape | solution.py:115
  535.7 5.1 collective-permute-start.123
  (379 shorter events, 415.1 us)
Async XLA Ops:
  13.8 9.3 %collective-permute-start.4 = (f32[14,18,1]{2,1,0:T(8,128)S(1)}, f32[14,18,1]{2,1,0:T(8,128)S(1)}, u32[]{:S(2)}, u32[]{:S(2)}) collective-permute-start(f32[14,18,1]{2,1,0:T(8,128)S(1)} %get-tuple-element.42), channel_id=1, source_target_pairs={{1,0},{2,1},{3,2},{5,4},{6,5},{7,6},{9,8},{10,9},{11,10},{13,12},{... | collective-permute-start | bytes 3032 | tf_op jit(solution)/shard_map/ppermute | solution.py:25
  15.1 9.7 %collective-permute-start.5 = (f32[14,18,1]{2,1,0:T(8,128)S(1)}, f32[14,18,1]{2,1,0:T(8,128)S(1)}, u32[]{:S(2)}, u32[]{:S(2)}) collective-permute-start(f32[14,18,1]{2,1,0:T(8,128)S(1)} %get-tuple-element.43), channel_id=1, source_target_pairs={{0,1},{1,2},{2,3},{4,5},{5,6},{6,7},{8,9},{9,10},{10,11},{12,13},{... | collective-permute-start | bytes 3032 | tf_op jit(solution)/shard_map/ppermute | solution.py:23
  38.4 8.6 %collective-permute-start.10 = (f32[14,18,1]{2,1,0:T(8,128)S(1)}, f32[14,18,1]{2,1,0:T(8,128)S(1)}, u32[]{:S(2)}, u32[]{:S(2)}) collective-permute-start(f32[14,18,1]{2,1,0:T(8,128)S(1)} %get-tuple-element.40), channel_id=1, source_target_pairs={{1,0},{2,1},{3,2},{5,4},{6,5},{7,6},{9,8},{10,9},{11,10},{13,12},{... | collective-permute-start | bytes 3032 | tf_op jit(solution)/shard_map/ppermute | solution.py:25
  39.7 9.1 %collective-permute-start.11 = (f32[14,18,1]{2,1,0:T(8,128)S(1)}, f32[14,18,1]{2,1,0:T(8,128)S(1)}, u32[]{:S(2)}, u32[]{:S(2)}) collective-permute-start(f32[14,18,1]{2,1,0:T(8,128)S(1)} %get-tuple-element.41), channel_id=1, source_target_pairs={{0,1},{1,2},{2,3},{4,5},{5,6},{6,7},{8,9},{9,10},{10,11},{12,13},{... | collective-permute-start | bytes 3032 | tf_op jit(solution)/shard_map/ppermute | solution.py:23
  199.2 7.4 %collective-permute-start.46 = (f32[14,18,1]{2,1,0:T(8,128)S(1)}, f32[14,18,1]{2,1,0:T(8,128)S(1)}, u32[]{:S(2)}, u32[]{:S(2)}) collective-permute-start(f32[14,18,1]{2,1,0:T(8,128)S(1)} %get-tuple-element.38), channel_id=1, source_target_pairs={{1,0},{2,1},{3,2},{5,4},{6,5},{7,6},{9,8},{10,9},{11,10},{13,12},{... | collective-permute-start | bytes 3032 | tf_op jit(solution)/shard_map/ppermute | solution.py:25
  200.5 7.5 %collective-permute-start.47 = (f32[14,18,1]{2,1,0:T(8,128)S(1)}, f32[14,18,1]{2,1,0:T(8,128)S(1)}, u32[]{:S(2)}, u32[]{:S(2)}) collective-permute-start(f32[14,18,1]{2,1,0:T(8,128)S(1)} %get-tuple-element.39), channel_id=1, source_target_pairs={{0,1},{1,2},{2,3},{4,5},{5,6},{6,7},{8,9},{9,10},{10,11},{12,13},{... | collective-permute-start | bytes 3032 | tf_op jit(solution)/shard_map/ppermute | solution.py:23
  222.8 7.5 %collective-permute-start.52 = (f32[14,18,1]{2,1,0:T(8,128)S(1)}, f32[14,18,1]{2,1,0:T(8,128)S(1)}, u32[]{:S(2)}, u32[]{:S(2)}) collective-permute-start(f32[14,18,1]{2,1,0:T(8,128)S(1)} %get-tuple-element.36), channel_id=1, source_target_pairs={{1,0},{2,1},{3,2},{5,4},{6,5},{7,6},{9,8},{10,9},{11,10},{13,12},{... | collective-permute-start | bytes 3032 | tf_op jit(solution)/shard_map/ppermute | solution.py:25
  224.1 7.6 %collective-permute-start.53 = (f32[14,18,1]{2,1,0:T(8,128)S(1)}, f32[14,18,1]{2,1,0:T(8,128)S(1)}, u32[]{:S(2)}, u32[]{:S(2)}) collective-permute-start(f32[14,18,1]{2,1,0:T(8,128)S(1)} %get-tuple-element.37), channel_id=1, source_target_pairs={{0,1},{1,2},{2,3},{4,5},{5,6},{6,7},{8,9},{9,10},{10,11},{12,13},{... | collective-permute-start | bytes 3032 | tf_op jit(solution)/shard_map/ppermute | solution.py:23
  246.5 7.5 %collective-permute-start.58 = (f32[14,18,1]{2,1,0:T(8,128)S(1)}, f32[14,18,1]{2,1,0:T(8,128)S(1)}, u32[]{:S(2)}, u32[]{:S(2)}) collective-permute-start(f32[14,18,1]{2,1,0:T(8,128)S(1)} %get-tuple-element.34), channel_id=1, source_target_pairs={{1,0},{2,1},{3,2},{5,4},{6,5},{7,6},{9,8},{10,9},{11,10},{13,12},{... | collective-permute-start | bytes 3032 | tf_op jit(solution)/shard_map/ppermute | solution.py:25
  247.8 7.6 %collective-permute-start.59 = (f32[14,18,1]{2,1,0:T(8,128)S(1)}, f32[14,18,1]{2,1,0:T(8,128)S(1)}, u32[]{:S(2)}, u32[]{:S(2)}) collective-permute-start(f32[14,18,1]{2,1,0:T(8,128)S(1)} %get-tuple-element.35), channel_id=1, source_target_pairs={{0,1},{1,2},{2,3},{4,5},{5,6},{6,7},{8,9},{9,10},{10,11},{12,13},{... | collective-permute-start | bytes 3032 | tf_op jit(solution)/shard_map/ppermute | solution.py:23
  270.5 12.7 %collective-permute-start.64 = (f32[3,14,18,1]{3,2,1,0:T(8,128)S(1)}, f32[3,14,18,1]{3,2,1,0:T(8,128)S(1)}, u32[]{:S(2)}, u32[]{:S(2)}) collective-permute-start(f32[3,14,18,1]{3,2,1,0:T(8,128)S(1)} %get-tuple-element.13), channel_id=1, source_target_pairs={{1,0},{2,1},{3,2},{5,4},{6,5},{7,6},{9,8},{10,9},{11,10},{13,12},{... | collective-permute-start | bytes 9080 | tf_op jit(solution)/shard_map/ppermute | solution.py:25
  271.8 13.2 %collective-permute-start.65 = (f32[3,14,18,1]{3,2,1,0:T(8,128)S(1)}, f32[3,14,18,1]{3,2,1,0:T(8,128)S(1)}, u32[]{:S(2)}, u32[]{:S(2)}) collective-permute-start(f32[3,14,18,1]{3,2,1,0:T(8,128)S(1)} %get-tuple-element.14), channel_id=1, source_target_pairs={{0,1},{1,2},{2,3},{4,5},{5,6},{6,7},{8,9},{9,10},{10,11},{12,13},{... | collective-permute-start | bytes 9080 | tf_op jit(solution)/shard_map/ppermute | solution.py:23
  300.4 11.6 %collective-permute-start.70 = (f32[3,14,18,1]{3,2,1,0:T(8,128)S(1)}, f32[3,14,18,1]{3,2,1,0:T(8,128)S(1)}, u32[]{:S(2)}, u32[]{:S(2)}) collective-permute-start(f32[3,14,18,1]{3,2,1,0:T(8,128)S(1)} %get-tuple-element.11), channel_id=1, source_target_pairs={{1,0},{2,1},{3,2},{5,4},{6,5},{7,6},{9,8},{10,9},{11,10},{13,12},{... | collective-permute-start | bytes 9080 | tf_op jit(solution)/shard_map/ppermute | solution.py:25
  301.7 12.0 %collective-permute-start.71 = (f32[3,14,18,1]{3,2,1,0:T(8,128)S(1)}, f32[3,14,18,1]{3,2,1,0:T(8,128)S(1)}, u32[]{:S(2)}, u32[]{:S(2)}) collective-permute-start(f32[3,14,18,1]{3,2,1,0:T(8,128)S(1)} %get-tuple-element.12), channel_id=1, source_target_pairs={{0,1},{1,2},{2,3},{4,5},{5,6},{6,7},{8,9},{9,10},{10,11},{12,13},{... | collective-permute-start | bytes 9080 | tf_op jit(solution)/shard_map/ppermute | solution.py:23
  321.1 7.7 %collective-permute-start.74 = (f32[14,1,128]{2,1,0:T(1,128)S(1)}, f32[14,1,128]{2,1,0:T(1,128)S(1)}, u32[]{:S(2)}, u32[]{:S(2)}) collective-permute-start(f32[14,1,128]{2,1,0:T(1,128)S(1)} %get-tuple-element.51), channel_id=1, source_target_pairs={{4,0},{8,4},{12,8},{5,1},{9,5},{13,9},{6,2},{10,6},{14,10},{7,3},{... | collective-permute-start | bytes 21512 | tf_op jit(solution)/shard_map/ppermute | solution.py:25
  329.8 7.5 %collective-permute-start.76 = (f32[14,18,1]{2,1,0:T(8,128)S(1)}, f32[14,18,1]{2,1,0:T(8,128)S(1)}, u32[]{:S(2)}, u32[]{:S(2)}) collective-permute-start(f32[14,18,1]{2,1,0:T(8,128)S(1)} %get-tuple-element.32), channel_id=1, source_target_pairs={{1,0},{2,1},{3,2},{5,4},{6,5},{7,6},{9,8},{10,9},{11,10},{13,12},{... | collective-permute-start | bytes 3032 | tf_op jit(solution)/shard_map/ppermute | solution.py:25
  331.1 7.6 %collective-permute-start.77 = (f32[14,18,1]{2,1,0:T(8,128)S(1)}, f32[14,18,1]{2,1,0:T(8,128)S(1)}, u32[]{:S(2)}, u32[]{:S(2)}) collective-permute-start(f32[14,18,1]{2,1,0:T(8,128)S(1)} %get-tuple-element.33), channel_id=1, source_target_pairs={{0,1},{1,2},{2,3},{4,5},{5,6},{6,7},{8,9},{9,10},{10,11},{12,13},{... | collective-permute-start | bytes 3032 | tf_op jit(solution)/shard_map/ppermute | solution.py:23
  346.1 8.7 %collective-permute-start.80 = (f32[14,1,128]{2,1,0:T(1,128)S(1)}, f32[14,1,128]{2,1,0:T(1,128)S(1)}, u32[]{:S(2)}, u32[]{:S(2)}) collective-permute-start(f32[14,1,128]{2,1,0:T(1,128)S(1)} %get-tuple-element.49), channel_id=1, source_target_pairs={{4,0},{8,4},{12,8},{5,1},{9,5},{13,9},{6,2},{10,6},{14,10},{7,3},{... | collective-permute-start | bytes 21512 | tf_op jit(solution)/shard_map/ppermute | solution.py:25
  347.4 8.3 %collective-permute-start.81 = (f32[14,1,128]{2,1,0:T(1,128)S(1)}, f32[14,1,128]{2,1,0:T(1,128)S(1)}, u32[]{:S(2)}, u32[]{:S(2)}) collective-permute-start(f32[14,1,128]{2,1,0:T(1,128)S(1)} %get-tuple-element.48), channel_id=1, source_target_pairs={{0,4},{4,8},{8,12},{1,5},{5,9},{9,13},{2,6},{6,10},{10,14},{3,7},{... | collective-permute-start | bytes 21512 | tf_op jit(solution)/shard_map/ppermute | solution.py:23
  355.8 7.6 %collective-permute-start.82 = (f32[14,18,1]{2,1,0:T(8,128)S(1)}, f32[14,18,1]{2,1,0:T(8,128)S(1)}, u32[]{:S(2)}, u32[]{:S(2)}) collective-permute-start(f32[14,18,1]{2,1,0:T(8,128)S(1)} %get-tuple-element.30), channel_id=1, source_target_pairs={{1,0},{2,1},{3,2},{5,4},{6,5},{7,6},{9,8},{10,9},{11,10},{13,12},{... | collective-permute-start | bytes 3032 | tf_op jit(solution)/shard_map/ppermute | solution.py:25
  357.1 7.8 %collective-permute-start.83 = (f32[14,18,1]{2,1,0:T(8,128)S(1)}, f32[14,18,1]{2,1,0:T(8,128)S(1)}, u32[]{:S(2)}, u32[]{:S(2)}) collective-permute-start(f32[14,18,1]{2,1,0:T(8,128)S(1)} %get-tuple-element.31), channel_id=1, source_target_pairs={{0,1},{1,2},{2,3},{4,5},{5,6},{6,7},{8,9},{9,10},{10,11},{12,13},{... | collective-permute-start | bytes 3032 | tf_op jit(solution)/shard_map/ppermute | solution.py:23
  519.5 7.5 %collective-permute-start.119 = (f32[14,18,1]{2,1,0:T(8,128)S(1)}, f32[14,18,1]{2,1,0:T(8,128)S(1)}, u32[]{:S(2)}, u32[]{:S(2)}) collective-permute-start(f32[14,18,1]{2,1,0:T(8,128)S(1)} %get-tuple-element.29), channel_id=1, source_target_pairs={{0,1},{1,2},{2,3},{4,5},{5,6},{6,7},{8,9},{9,10},{10,11},{12,13},{... | collective-permute-start | bytes 3032 | tf_op jit(solution)/shard_map/ppermute | solution.py:23
  541.7 7.5 %collective-permute-start.124 = (f32[14,18,1]{2,1,0:T(8,128)S(1)}, f32[14,18,1]{2,1,0:T(8,128)S(1)}, u32[]{:S(2)}, u32[]{:S(2)}) collective-permute-start(f32[14,18,1]{2,1,0:T(8,128)S(1)} %get-tuple-element.26), channel_id=1, source_target_pairs={{1,0},{2,1},{3,2},{5,4},{6,5},{7,6},{9,8},{10,9},{11,10},{13,12},{... | collective-permute-start | bytes 3032 | tf_op jit(solution)/shard_map/ppermute | solution.py:25
  543.0 7.6 %collective-permute-start.125 = (f32[14,18,1]{2,1,0:T(8,128)S(1)}, f32[14,18,1]{2,1,0:T(8,128)S(1)}, u32[]{:S(2)}, u32[]{:S(2)}) collective-permute-start(f32[14,18,1]{2,1,0:T(8,128)S(1)} %get-tuple-element.27), channel_id=1, source_target_pairs={{0,1},{1,2},{2,3},{4,5},{5,6},{6,7},{8,9},{9,10},{10,11},{12,13},{... | collective-permute-start | bytes 3032 | tf_op jit(solution)/shard_map/ppermute | solution.py:23
  (104 other events, 710.3 us)
where the time goes:
time: 561 us; the launch traced here: 551 us
  starting transfers between devices  366 us (65%)
  waiting for transfers between devices  130 us (23%)
  local copies, waits for them, and re-layouts  38.6 us (7%)
  other arithmetic  15.4 us (3%)
    ppermute x63, starting transfers between devices, with_halo(): lax.ppermute(tail, axis, [(i, (i + 1) % count) for i in range(ends)])  284 us
    ppermute x63, starting transfers between devices, with_halo(): lax.ppermute(head, axis, [((i + 1) % count, i) for i in range(ends)])  81.5 us
    ppermute x63, waiting for transfers between devices, with_halo(): lax.ppermute(tail, axis, [(i, (i + 1) % count) for i in range(ends)])  71.7 us
    ppermute x63, waiting for transfers between devices, with_halo(): lax.ppermute(head, axis, [((i + 1) % count, i) for i in range(ends)])  58.1 us
    reshape x4, local copies, waits for them, and re-layouts, restrict(): values.reshape(extent_x // 2, 2, extent_y // 2, 2, extent_z // 2, 2)  17 us
    reshape x4, local copies, waits for them, and re-layouts, prolong(): return spread.reshape(2 * extent_x, 2 * extent_y, 2 * extent_z)  12 us
  transfers between devices with their start and end apart: 126, of which 84 were waited for; matrix products, arithmetic and copies ran while one was open for 0% of the time, Pallas kernels for 0%

commit v1 on v0

v1 whole, which is shorter than its diff:
```python
import functools

import jax
import jax.numpy as jnp
from jax import lax
from jax.experimental import pallas as pl
from jax.experimental.pallas import tpu as pltpu
from jax.sharding import PartitionSpec as P

MESH = pl.DeviceIdType.MESH
OMEGA = 0.8
KEEP = 1.0 - OMEGA
CS = OMEGA / 6.0
H = 8
HW = 3
ZS = 8
L1S = 16
UNROLL = 2


def loop(low, high, step, unroll=UNROLL):
    def run(p, carry):
        step(p)
        return carry

    lax.fori_loop(low, high, run, 0, unroll=min(unroll, high - low))


def kernel(
    counts, local,
    p_ref, w_ref, o_ref,
    pr, va, vb, vel, flux, wr, m2, bz, wzr, pk, wpk,
    s16, cat, b1, v1, r1, b2, u2, e1, tmp, ex, tall,
    m1s, m2s, m1r, m2r, fs, fr,
    psend, precv, wsend, wrecv, gsend, grecv, fsend, frecv,
):
    gx, gy, gz = counts
    nx, ny, nz = local
    cx, cy, cz = nx // 2, ny // 2, nz // 2
    mx, my, mz = lax.axis_index("gx"), lax.axis_index("gy"), lax.axis_index("gz")
    me = mx * gy + my
    group = gx * gy

    def exists(dx, dy, dz):
        ok = None
        for d, m, g in ((dx, mx, gx), (dy, my, gy), (dz, mz, gz)):
            if d:
                here = (m + d >= 0) & (m + d < g)
                ok = here if ok is None else ok & here
        return ok

    barrier = pltpu.get_barrier_semaphore()

    def peers(act):
        def at(t):
            ax, ay = t // gy, t % gy
            for dz in (-1, 0, 1):
                ok = (mz + dz >= 0) & (mz + dz < gz)
                if dz == 0:
                    ok = t != me

                @pl.when(ok)
                def _():
                    act(t, ax, ay, dz)

        loop(0, group, at, 1)

    peers(lambda t, ax, ay, dz: pl.semaphore_signal(
        barrier, inc=1, device_id=(ax, ay, mz + dz), device_id_type=MESH))

    row = lax.broadcasted_iota(jnp.int32, (ny + 2 * H, 2 * nz), 0) - H
    lane = lax.broadcasted_iota(jnp.int32, (ny + 2 * H, 2 * nz), 1)
    zpos = jnp.where(lane < nz + nz // 2, lane, lane - 2 * nz)
    inside = (
        (row + my * ny >= 0) & (row + my * ny < gy * ny)
        & (zpos + mz * nz >= 0) & (zpos + mz * nz < gz * nz)
    )
    m2[...] = inside.astype(jnp.float32)

    def sx(p):
        x = mx * nx + p - H
        return jnp.where((x >= 0) & (x < gx * nx), 1.0, 0.0).astype(jnp.float32)

    lane1 = lax.broadcasted_iota(jnp.int32, (ny, nz), 1)
    lo, hi = jnp.zeros((ny, nz), jnp.float32), jnp.zeros((ny, nz), jnp.float32)
    for i in range(nx):
        plane = p_ref[i]
        a = plane if i == 0 else pltpu.roll(plane, ZS * i, 1)
        b = pltpu.roll(plane, (ZS * (i + 1)) % nz, 1)
        sel = (lane1 >= ZS * i) & (lane1 < ZS * (i + 1))
        lo = jnp.where(sel, a, lo)
        hi = jnp.where(sel, b, hi)
    pk[0] = lo
    pk[1] = hi
    lo, hi = jnp.zeros((ny, nz), jnp.float32), jnp.zeros((ny, nz), jnp.float32)
    for e in range(3):
        for i in range(nx):
            at = HW * (e * nx + i)
            plane = w_ref[e, i]
            a = plane if at == 0 else pltpu.roll(plane, at, 1)
            b = pltpu.roll(plane, (at + HW) % nz, 1)
            sel = (lane1 >= at) & (lane1 < at + HW)
            lo = jnp.where(sel, a, lo)
            hi = jnp.where(sel, b, hi)
    wpk[0] = lo
    wpk[1] = hi

    n_peers = 3 * group - 1
    n_peers = n_peers - jnp.where(mz == 0, group, 0) - jnp.where(mz == gz - 1, group, 0)
    pl.semaphore_wait(barrier, n_peers)

    def span(d, n, h, big):
        if d == 0:
            return pl.ds(0, n), pl.ds(big, n)
        if d > 0:
            return pl.ds(n - h, h), pl.ds(0, h)
        return pl.ds(0, h), pl.ds(big + n, h)

    offsets = [
        (dx, dy, dz) for dz in (0, -1, 1) for dx in (0, -1, 1) for dy in (0, -1, 1)
        if (dx, dy, dz) != (0, 0, 0)
        and (gx > 1 or dx == 0) and (gy > 1 or dy == 0) and (gz > 1 or dz == 0)
    ]

    def key(d):
        return (d[0] + 1) * 9 + (d[1] + 1) * 3 + d[2] + 1

    def pcopy(d):
        dx, dy, dz = d
        to = (mx + dx, my + dy, mz + dz)
        k = key(d)
        if dz == 0:
            xs, xd = span(dx, nx, H, H)
            ys, yd = span(dy, ny, H, H)
            src, dst = p_ref.at[xs, ys], pr.at[xd, yd, pl.ds(0, nz)]
        else:
            src = pk.at[0 if dz < 0 else 1]
            dst = bz.at[0 if dz < 0 else 1, (1 - dx) * 3 + 1 - dy]
        return pltpu.make_async_remote_copy(
            src_ref=src, dst_ref=dst, send_sem=psend.at[k], recv_sem=precv.at[k],
            device_id=to, device_id_type=MESH)

    def wcopy(d):
        dx, dy, dz = d
        to = (mx + dx, my + dy, mz + dz)
        k = key(d)
        if dz == 0:
            xs, xd = span(dx, nx, HW, HW)
            ys, yd = span(dy, ny, H, H)
            src, dst = w_ref.at[:, xs, ys], wr.at[:, xd, yd, pl.ds(0, nz)]
        else:
            src = wpk.at[0 if dz < 0 else 1]
            dst = wzr.at[0 if dz < 0 else 1, (1 - dx) * 3 + 1 - dy]
        return pltpu.make_async_remote_copy(
            src_ref=src, dst_ref=dst, send_sem=wsend.at[k], recv_sem=wrecv.at[k],
            device_id=to, device_id_type=MESH)

    def opposite(d):
        return (-d[0], -d[1], -d[2])

    for d in offsets:
        pl.when(exists(*d))(lambda d=d: pcopy(d).start())
    for d in offsets:
        pl.when(exists(*d))(lambda d=d: wcopy(d).start())

    pr[H : H + nx, H : H + ny, 0:nz] = p_ref[...]
    wr[:, HW : HW + nx, H : H + ny, 0:nz] = w_ref[...]

    for d in offsets:
        pl.when(exists(*opposite(d)))(lambda d=d: pcopy(d).wait_recv())

    lane_h = lax.broadcasted_iota(jnp.int32, (ny + 2 * H, nz), 1)

    def rows_of(buf, side, ix, comp=None):
        parts = []
        for iy, (s, n) in enumerate(((ny - H, H), (0, ny), (0, H))):
            parts.append(buf[side, ix * 3 + iy, pl.ds(s, n), :])
        return jnp.concatenate(parts, axis=0)

    def clean(buf_lo, buf_hi, at, width):
        right = buf_lo if at == 0 else pltpu.roll(buf_lo, nz - at, 1)
        left = pltpu.roll(buf_hi, (2 * nz - width - at) % nz, 1)
        return jnp.where(lane_h < width, right, jnp.where(lane_h >= nz - width, left, 0.0))

    okmask = m2[...] > 0.5
    for ix, (first, low, n) in enumerate(((nx - H, 0, H), (0, H, nx), (0, H + nx, H))):
        right, left = rows_of(bz, 0, ix), rows_of(bz, 1, ix)
        for i in range(n):
            p = low + i
            halo = clean(right, left, ZS * (first + i), ZS)
            x = mx * nx + p - H
            good = okmask & ((x >= 0) & (x < gx * nx))
            pr[p, :, 0:nz] = jnp.where(good[:, :nz], pr[p, :, 0:nz], 0.0)
            pr[p, :, nz:] = jnp.where(good[:, nz:], halo, 0.0)

    ry, rz = ny + 2 * H, 2 * nz

    def up(v, axis, k=1):
        return pltpu.roll(v, v.shape[axis] - k, axis)

    def down(v, axis, k=1):
        return pltpu.roll(v, k, axis)

    def six(ref, p, centre):
        return (
            (ref[p + 1] + ref[p - 1])
            + (up(centre, 0) + down(centre, 0))
            + (up(centre, 1) + down(centre, 1))
        )

    CB0 = OMEGA / 6.0

    def pre(src, dst, low, high):
        def at(p):
            c = src[p]
            dst[p] = (CB0 * (1.2 * c + CS * six(src, p, c))) * (sx(p) * m2[...])

        loop(low, high, at)

    li = lax.broadcasted_iota(jnp.int32, (nz, nz), 0)
    lj = lax.broadcasted_iota(jnp.int32, (nz, nz), 1)
    squeeze = jnp.where(li // 2 == lj % cz, 0.125, 0.0).astype(jnp.float32)
    ei = lax.broadcasted_iota(jnp.int32, (nz, 2 * nz), 0)
    ej = lax.broadcasted_iota(jnp.int32, (nz, 2 * nz), 1)
    spread = jnp.where(ej // 2 == ei, 1.0, 0.0).astype(jnp.float32)

    lane8 = lax.broadcasted_iota(jnp.int32, (cy, nz), 1)
    z1 = jnp.where(lane8 < nz - cz // 2, lane8, lane8 - nz)
    zin1 = (
        (z1 + mz * cz >= 0) & (z1 + mz * cz < gz * cz)
        & (z1 >= -L1S) & (z1 < cz + L1S)
    )
    tr = 8 + gy * cy
    row1 = lax.broadcasted_iota(jnp.int32, (tr, nz), 0)
    lan1 = lax.broadcasted_iota(jnp.int32, (tr, nz), 1)
    zl1 = jnp.where(lan1 < nz - cz // 2, lan1, lan1 - nz)
    mask1 = (
        (row1 >= 4) & (row1 < tr - 4)
        & (zl1 + mz * cz >= 0) & (zl1 + mz * cz < gz * cz)
    ).astype(jnp.float32)
    hy = gy * cy // 2
    row2 = lax.broadcasted_iota(jnp.int32, (hy, nz), 0)
    lan2 = lax.broadcasted_iota(jnp.int32, (hy, nz), 1)
    zl2 = jnp.where(lan2 < nz - cz // 2, lan2, lan2 - nz)
    mask2 = ((zl2 + mz * cz >= 0) & (zl2 + mz * cz < gz * cz)).astype(jnp.float32)
    not_first = (row2 > 0).astype(jnp.float32)
    not_last = (row2 < hy - 1).astype(jnp.float32)
    even2 = lan2 % 2 == 0

    X1 = gx * cx
    X2 = X1 // 2
    zero1 = jnp.zeros((tr, nz), jnp.float32)
    zero2 = jnp.zeros((hy, nz), jnp.float32)
    for ref in (b1, v1, r1, e1):
        ref[0] = zero1
        ref[X1 + 1] = zero1
    loop(1, X1 + 1, lambda p: b1.__setitem__(p, zero1))
    u2[0, 0] = zero2
    u2[0, X2 + 1] = zero2
    u2[1, 0] = zero2
    u2[1, X2 + 1] = zero2

    def gcopy(turn, t, ax, ay, dz, slot):
        side = dz + 1
        if dz == 0:
            src, dst = m1s.at[turn], m1r.at[turn, slot]
        else:
            src = m2s.at[turn, 0 if dz < 0 else 1]
            dst = m2r.at[turn, slot, 0 if dz < 0 else 1]
        return pltpu.make_async_remote_copy(
            src_ref=src, dst_ref=dst, send_sem=gsend.at[turn, t, side],
            recv_sem=grecv.at[turn, slot, side],
            device_id=(ax, ay, mz + dz), device_id_type=MESH)

    def coarse_source(turn, src, v):
        for i in range(cx):
            parts = []
            for q in (H + 2 * i, H + 2 * i + 1):
                c = v[q]
                r = src[q] - 6.0 * c + six(v, q, c)
                parts.append(r[H : H + ny, 0:nz])
            s16[i] = parts[0] + parts[1]
            cat[cy * i : cy * (i + 1)] = (
                s16[i, pl.ds(0, cy, stride=2), :] + s16[i, pl.ds(1, cy, stride=2), :]
            )
        c1 = lax.dot_general(
            cat[...], squeeze, (((1,), (0,)), ((), ())),
            precision=lax.Precision.HIGHEST, preferred_element_type=jnp.float32)
        planes = [c1[cy * i : cy * (i + 1)] for i in range(cx)]
        for i in range(cx // 2):
            m1s[turn, i] = jnp.where(lane8 < cz, planes[i], planes[i + cx // 2])
            m1r[turn, me, i] = jnp.where(lane8 < cz, planes[i], planes[i + cx // 2])
        lo = jnp.zeros((cy, nz), jnp.float32)
        hi = jnp.zeros((cy, nz), jnp.float32)
        for i in range(cx):
            sel = (lane8 >= L1S * i) & (lane8 < L1S * (i + 1))
            a = planes[i] if i == 0 else pltpu.roll(planes[i], L1S * i, 1)
            b = pltpu.roll(planes[i], (L1S * i + nz - cz + L1S) % nz, 1)
            lo = jnp.where(sel, a, lo)
            hi = jnp.where(sel, b, hi)
        m2s[turn, 0] = lo
        m2s[turn, 1] = hi
        peers(lambda t, ax, ay, dz: gcopy(turn, t, ax, ay, dz, me).start())

    def coarse_gather(turn):
        def at(t):
            ax, ay = t // gy, t % gy
            for dz in (-1, 0, 1):
                ok = (mz - dz >= 0) & (mz - dz < gz)
                if dz == 0:
                    ok = t != me

                @pl.when(ok)
                def _():
                    gcopy(turn, t, ax, ay, dz, t).wait_recv()

        loop(0, group, at, 1)
        for t in range(group):
            ax, ay = t // gy, t % gy
            for i in range(cx):
                body = m1r[turn, t, i % (cx // 2)]
                if i >= cx // 2:
                    body = pltpu.roll(body, cz, 1)
                right = pltpu.roll(m2r[turn, t, 0], (cz - L1S * i) % nz, 1)
                left = pltpu.roll(m2r[turn, t, 1], (2 * nz - L1S - L1S * i) % nz, 1)
                whole = jnp.where(lane8 < cz, body, jnp.where(lane8 < nz - L1S, right, left))
                b1[1 + ax * cx + i, 4 + cy * ay : 4 + cy * (ay + 1)] = jnp.where(zin1, whole, 0.0)

    def coarse(turn):
        cb1 = OMEGA / (6.0 * 0.25)
        cb2 = OMEGA / (6.0 * 0.0625)

        def at(p):
            c = b1[p]
            v1[p] = (cb1 * (1.2 * c + CS * six(b1, p, c))) * mask1

        loop(1, X1 + 1, at)

        def residual(p):
            c = v1[p]
            return b1[p] - 0.25 * (6.0 * c - six(v1, p, c))

        def down_to_2(j):
            tall[...] = residual(2 * j + 1) + residual(2 * j + 2)
            s = tall[pl.ds(4, hy, stride=2), :] + tall[pl.ds(5, hy, stride=2), :]
            s = s + jnp.where(even2, up(s, 1), down(s, 1))
            s = (0.125 * s) * mask2
            b2[j + 1] = s
            u2[0, j + 1] = cb2 * s

        loop(0, X2, down_to_2)
        for number in range(3):
            a, b = number % 2, (number + 1) % 2

            def sweep2(j, a=a, b=b):
                c = u2[a, j]
                s = (
                    (u2[a, j + 1] + u2[a, j - 1])
                    + (up(c, 0) * not_last + down(c, 0) * not_first)
                    + (up(c, 1, 2) + down(c, 1, 2))
                )
                u2[b, j] = (KEEP * c + cb2 * b2[j] + CS * s) * mask2

            loop(1, X2 + 1, sweep2)

        tall[...] = zero1

        def up_to_1(j):
            e = u2[1, j + 1]
            tall[pl.ds(4, hy, stride=2), :] = e
            tall[pl.ds(5, hy, stride=2), :] = e
            t = tall[...]
            v1[2 * j + 1] = v1[2 * j + 1] + t
            v1[2 * j + 2] = v1[2 * j + 2] + t

        loop(0, X2, up_to_1)
        for src, dst in ((v1, r1), (r1, e1)):
            def sweep1(p, src=src, dst=dst):
                c = src[p]
                dst[p] = (KEEP * c + cb1 * b1[p] + CS * six(src, p, c)) * mask1

            loop(1, X1 + 1, sweep1)

    half = ry // 2

    def correct(v, low, high):
        first = low // 2
        last = (high + 1) // 2
        n = last - first
        for k in range(n):
            x = mx * cx + first + k - H // 2
            x = jnp.clip(x, 0, X1 - 1) + 1
            ex[half * k : half * (k + 1)] = e1[x, pl.ds(pl.multiple_of(my * cy, 8), half), :]
        wide = lax.dot_general(
            ex[0 : half * n], spread, (((1,), (0,)), ((), ())),
            precision=lax.Precision.HIGHEST, preferred_element_type=jnp.float32)
        m = m2[...]
        for k in range(n):
            piece = wide[half * k : half * (k + 1)]
            for h in range(2):
                tmp[k, h, pl.ds(0, half, stride=2), :] = piece[:, h * nz : (h + 1) * nz]
                tmp[k, h, pl.ds(1, half, stride=2), :] = piece[:, h * nz : (h + 1) * nz]
            for q in (2 * (first + k), 2 * (first + k) + 1):
                if low <= q < high:
                    for h in range(2):
                        ls = slice(h * nz, (h + 1) * nz)
                        v[q, :, ls] = v[q, :, ls] + tmp[k, h] * (sx(q) * m[:, ls])

    def post(b, src, dst, low, high):
        def at(p):
            c = src[p]
            dst[p] = (KEEP * c + CB0 * b[p] + CS * six(src, p, c)) * (sx(p) * m2[...])

        loop(low, high, at)

    pre(pr, va, 1, nx + 2 * H - 1)
    coarse_source(0, pr, va)
    coarse_gather(0)
    coarse(0)
    correct(va, 1, nx + 2 * H - 1)
    post(pr, va, vb, 2, nx + 2 * H - 2)
    post(pr, vb, va, 3, nx + 2 * H - 3)

    def velocity(p):
        c = va[p]
        m = (0.5 * sx(p)) * m2[...]
        vel[0, p] = (va[p + 1] - va[p - 1]) * m
        vel[1, p] = (up(c, 0) - down(c, 0)) * m
        vel[2, p] = (up(c, 1) - down(c, 1)) * m

    loop(4, nx + 2 * H - 4, velocity)

    for d in offsets:
        pl.when(exists(*opposite(d)))(lambda d=d: wcopy(d).wait_recv())
    for ix, (first, low, n) in enumerate(((nx - HW, 0, HW), (0, HW, nx), (0, HW + nx, HW))):
        right, left = rows_of(wzr, 0, ix), rows_of(wzr, 1, ix)
        for e in range(3):
            for i in range(n):
                p = low + i
                halo = clean(right, left, HW * (e * nx + first + i), HW)
                x = mx * nx + p - HW
                good = okmask & ((x >= 0) & (x < gx * nx))
                wr[e, p, :, 0:nz] = jnp.where(good[:, :nz], wr[e, p, :, 0:nz], 0.0)
                wr[e, p, :, nz:] = jnp.where(good[:, nz:], halo, 0.0)

    def momentum(p):
        m = sx(p) * m2[...]
        q = p - (H - HW)
        w0, w1, w2 = 0.5 * wr[0, q], 0.5 * wr[1, q], 0.5 * wr[2, q]
        for d in range(3):
            c, n, s = vel[d, p], vel[d, p + 1], vel[d, p - 1]
            yu, yd, zu, zd = up(c, 0), down(c, 0), up(c, 1), down(c, 1)
            total = ((n + s) + (yu + yd)) + (zu + zd)
            conv = w0 * (n - s) + w1 * (yu - yd) + w2 * (zu - zd)
            flux[d, p] = (7.0 * c - total + conv) * m

    loop(H - HW, H + nx + HW, momentum, 1)

    def product(p):
        f1, f2 = flux[1, p], flux[2, p]
        s = (flux[0, p + 1] - flux[0, p - 1]) + (up(f1, 0) - down(f1, 0)) + (up(f2, 1) - down(f2, 1))
        pr[p] = s * ((-0.5 * sx(p)) * m2[...])

    loop(H - 2, H + nx + 2, product)

    vb[H - 2] = jnp.zeros((ry, rz), jnp.float32)
    vb[H + nx + 1] = jnp.zeros((ry, rz), jnp.float32)
    pre(pr, vb, H - 1, H + nx + 1)

    fs[0] = vb[H + 1, H : H + ny, 0:nz]
    fs[1] = vb[H + nx - 2, H : H + ny, 0:nz]
    for i in range(nx):
        fs[2, i : i + 1] = vb[H + i, H + 1 : H + 2, 0:nz]
        fs[3, i : i + 1] = vb[H + i, H + ny - 2 : H + ny - 1, 0:nz]
    lo, hi = jnp.zeros((ny, nz), jnp.float32), jnp.zeros((ny, nz), jnp.float32)
    for i in range(nx):
        plane = vb[H + i, H : H + ny, 0:nz]
        lo = jnp.where(lane1 == i, pltpu.roll(plane, (nz + i - 1) % nz, 1), lo)
        hi = jnp.where(lane1 == i, pltpu.roll(plane, (i + 2) % nz, 1), hi)
    fs[4] = lo
    fs[5] = hi
    faces = [(-1, 0, 0), (1, 0, 0), (0, -1, 0), (0, 1, 0), (0, 0, -1), (0, 0, 1)]
    faces = [(k, d) for k, d in enumerate(faces) if d in offsets]

    def fcopy(k, d):
        return pltpu.make_async_remote_copy(
            src_ref=fs.at[k], dst_ref=fr.at[k], send_sem=fsend.at[k], recv_sem=frecv.at[k],
            device_id=(mx + d[0], my + d[1], mz + d[2]), device_id_type=MESH)

    coarse_source(1, pr, vb)
    for k, d in faces:
        pl.when(exists(*d))(lambda k=k, d=d: fcopy(k, d).start())
    coarse_gather(1)
    coarse(1)
    for k, d in faces:
        back = opposite(d)

        @pl.when(exists(*back))
        def _(k=k, d=d):
            fcopy(k, d).wait_recv()
            if k == 0:
                vb[H + nx + 1, H : H + ny, 0:nz] = fr[0]
            if k == 1:
                vb[H - 2, H : H + ny, 0:nz] = fr[1]
            if k == 2:
                for i in range(nx):
                    vb[H + i, H + ny + 1 : H + ny + 2, 0:nz] = fr[2, i : i + 1]
            if k == 3:
                for i in range(nx):
                    vb[H + i, H - 2 : H - 1, 0:nz] = fr[3, i : i + 1]
            if k == 4:
                for i in range(nx):
                    old = vb[H + i, H : H + ny, nz : 2 * nz]
                    new = pltpu.roll(fr[4], (nz + 1 - i) % nz, 1)
                    vb[H + i, H : H + ny, nz : 2 * nz] = jnp.where(lane1 == 1, new, old)
            if k == 5:
                for i in range(nx):
                    old = vb[H + i, H : H + ny, nz : 2 * nz]
                    new = pltpu.roll(fr[5], (nz - 2 - i) % nz, 1)
                    vb[H + i, H : H + ny, nz : 2 * nz] = jnp.where(lane1 == nz - 2, new, old)

    correct(vb, H - 2, H + nx + 2)
    post(pr, vb, va, H - 1, H + nx + 1)

    def finish(p):
        c = va[p]
        out = KEEP * c + CB0 * pr[p] + CS * six(va, p, c)
        o_ref[p - H] = out[H : H + ny, 0:nz]

    loop(H, H + nx, finish)

    for d in offsets:
        @pl.when(exists(*d))
        def _(d=d):
            pcopy(d).wait_send()
            wcopy(d).wait_send()
    peers(lambda t, ax, ay, dz: gcopy(0, t, ax, ay, dz, me).wait_send())
    peers(lambda t, ax, ay, dz: gcopy(1, t, ax, ay, dz, me).wait_send())
    for k, d in faces:
        pl.when(exists(*d))(lambda k=k, d=d: fcopy(k, d).wait_send())


def body(counts, pressure, wind):
    gx, gy, gz = counts
    nx, ny, nz = pressure.shape
    cx, cy = nx // 2, ny // 2
    rx, ry, rz = nx + 2 * H, ny + 2 * H, 2 * nz
    group = gx * gy
    x1, tr, hy = gx * cx, gy * cy + 8, gy * cy // 2
    V = lambda *shape: pltpu.VMEM(shape, jnp.float32)
    D = lambda *shape: pltpu.SemaphoreType.DMA(shape)
    scratch = [
        V(rx, ry, rz), V(rx, ry, rz), V(rx, ry, rz),
        V(3, rx, ry, rz), V(3, rx, ry, rz), V(3, nx + 2 * HW, ry, rz),
        V(ry, rz), V(2, 9, ny, nz), V(2, 9, ny, nz), V(2, ny, nz), V(2, ny, nz),
        V(cx, ny, nz), V(cx * cy, nz),
        V(x1 + 2, tr, nz), V(x1 + 2, tr, nz), V(x1 + 2, tr, nz),
        V(x1 // 2 + 2, hy, nz), V(2, x1 // 2 + 2, hy, nz), V(x1 + 2, tr, nz),
        V(rx // 2, 2, ry, nz), V(rx // 2 * (ry // 2), nz), V(tr, nz),
        V(2, cx // 2, cy, nz), V(2, 2, cy, nz),
        V(2, group, cx // 2, cy, nz), V(2, group, 2, cy, nz),
        V(6, ny, nz), V(6, ny, nz),
        D(27), D(27), D(27), D(27), D(2, group, 3), D(2, group, 3), D(6), D(6),
    ]
    return pl.pallas_call(
        functools.partial(kernel, counts, (nx, ny, nz)),
        out_shape=jax.ShapeDtypeStruct(pressure.shape, jnp.float32),
        in_specs=[pl.BlockSpec(memory_space=pltpu.VMEM)] * 2,
        out_specs=pl.BlockSpec(memory_space=pltpu.VMEM),
        scratch_shapes=scratch,
        compiler_params=pltpu.CompilerParams(collective_id=0, has_side_effects=True),
    )(pressure, wind)


def solution(mesh):
    counts = tuple(mesh.shape[name] for name in ("gx", "gy", "gz"))
    in_specs = (P("gx", "gy", "gz"), P(None, "gx", "gy", "gz"))
    return jax.shard_map(
        functools.partial(body, counts), mesh=mesh, in_specs=in_specs,
        out_specs=P("gx", "gy", "gz"), check_vma=False)
```

time: 561 us -> 45 us (0.08); the launches traced: 551 us -> 44.9 us
  starting transfers between devices: 366 us -> 0 us
  waiting for transfers between devices: 130 us -> 0 us
  Pallas kernels: 0 us -> 43.3 us
  local copies, waits for them, and re-layouts: 38.6 us -> 1.54 us
  other arithmetic: 15.4 us -> 0 us
    ppermute x126 -> x0, starting transfers between devices: 366 us -> none  [the longest x63 284 us: with_halo(): lax.ppermute(tail, axis, [(i, (i + 1) % count) for i in range(ends)])]
    ppermute x126 -> x0, waiting for transfers between devices: 130 us -> none  [the longest x63 71.7 us: with_halo(): lax.ppermute(tail, axis, [(i, (i + 1) % count) for i in range(ends)])]
    pallas_call x0 -> x1, Pallas kernels: none -> 43.3 us  [body(): pl.pallas_call(functools.partial(kernel, counts, (nx, ny, nz)), out_shape...]
    reshape x8 -> x0, local copies, waits for them, and re-layouts: 29 us -> none  [the longest x4 17 us: restrict(): values.reshape(extent_x // 2, 2, extent_y // 2, 2, extent_z // 2, 2)]
    broadcast_in_dim x4 -> x0, local copies, waits for them, and re-layouts: 7.38 us -> none  [prolong(): jnp.broadcast_to(values[:, None, :, None, :, None], (extent_x, 2, extent_...]
    reduce_sum x4 -> x0, other arithmetic: 6.84 us -> none  [restrict(): return 0.125 * jnp.sum(blocks, axis=(1, 3, 5))]
  transfers between devices with their start and end apart: 126 -> 0, of which waited for: 84 -> 0; matrix products, arithmetic and copies ran while one was open for 0% -> 0% of each run, Pallas kernels for 0% -> 0%
where the time goes in v1:
time: 45 us; the launch traced here: 44.9 us
  Pallas kernels  43.3 us (96%)
  local copies, waits for them, and re-layouts  1.54 us (3%)
    pallas_call x1, Pallas kernels, body(): pl.pallas_call(functools.partial(kernel, counts, (nx, ny, nz)), out_shape...  43.3 us
    unnamed x1, local copies, waits for them, and re-layouts  1.54 us

profile of v1, /device:TPU:0, one launch (start us, length us, event | category | flops | bytes accessed | tf_op | source)
XLA Modules:
  0.0 44.9 jit_solution(1130198263531266688)
XLA Ops:
  0.0 43.3 %shard_map.28 = f32[12,16,128]{2,1,0:T(8,128)} custom-call(f32[12,16,128]{2,1,0:T(8,128)} %p_ref.1, f32[3,12,16,128]{3,2,1,0:T(8,128)} %w_ref.1), custom_call_target="tpu_custom_call" | custom-call | tf_op jit(solution)/shard_map/pallas_call | solution.py:565
  43.3 1.5 %copy.4 = f32[12,16,128]{2,1,0:T(8,128)} copy(f32[12,16,128]{2,1,0:T(8,128)} %shard_map.28) | data formatting | bytes 196608

commit v2 on v1

--- a/solution.py
+++ b/solution.py
@@ -15,7 +15,8 @@
 HW = 3
 ZS = 8
 L1S = 16
-UNROLL = 2
+UNROLL = 6
+NEAR = 2
 
 
 def loop(low, high, step, unroll=UNROLL):
@@ -32,7 +33,7 @@
     pr, va, vb, vel, flux, wr, m2, bz, wzr, pk, wpk,
     s16, cat, b1, v1, r1, b2, u2, e1, tmp, ex, tall,
     m1s, m2s, m1r, m2r, fs, fr,
-    psend, precv, wsend, wrecv, gsend, grecv, fsend, frecv,
+    lsem, psend, precv, wsend, wrecv, gsend, grecv, fsend, frecv,
 ):
     gx, gy, gz = counts
     nx, ny, nz = local
@@ -48,6 +49,13 @@
                 here = (m + d >= 0) & (m + d < g)
                 ok = here if ok is None else ok & here
         return ok
+
+    own_p = pltpu.make_async_copy(
+        p_ref, pr.at[pl.ds(H, nx), pl.ds(H, ny), pl.ds(0, nz)], lsem.at[0])
+    own_w = pltpu.make_async_copy(
+        w_ref, wr.at[:, pl.ds(HW, nx), pl.ds(H, ny), pl.ds(0, nz)], lsem.at[1])
+    own_p.start()
+    own_w.start()
 
     barrier = pltpu.get_barrier_semaphore()
 
@@ -82,42 +90,34 @@
         return jnp.where((x >= 0) & (x < gx * nx), 1.0, 0.0).astype(jnp.float32)
 
     lane1 = lax.broadcasted_iota(jnp.int32, (ny, nz), 1)
-    lo, hi = jnp.zeros((ny, nz), jnp.float32), jnp.zeros((ny, nz), jnp.float32)
-    for i in range(nx):
-        plane = p_ref[i]
-        a = plane if i == 0 else pltpu.roll(plane, ZS * i, 1)
-        b = pltpu.roll(plane, (ZS * (i + 1)) % nz, 1)
-        sel = (lane1 >= ZS * i) & (lane1 < ZS * (i + 1))
-        lo = jnp.where(sel, a, lo)
-        hi = jnp.where(sel, b, hi)
-    pk[0] = lo
-    pk[1] = hi
-    lo, hi = jnp.zeros((ny, nz), jnp.float32), jnp.zeros((ny, nz), jnp.float32)
-    for e in range(3):
-        for i in range(nx):
-            at = HW * (e * nx + i)
-            plane = w_ref[e, i]
+
+    def pack(planes, width):
+        lo, hi = jnp.zeros((ny, nz), jnp.float32), jnp.zeros((ny, nz), jnp.float32)
+        for i, plane in enumerate(planes):
+            at = width * i
             a = plane if at == 0 else pltpu.roll(plane, at, 1)
-            b = pltpu.roll(plane, (at + HW) % nz, 1)
-            sel = (lane1 >= at) & (lane1 < at + HW)
+            b = pltpu.roll(plane, (at + width) % nz, 1)
+            sel = (lane1 >= at) & (lane1 < at + width)
             lo = jnp.where(sel, a, lo)
             hi = jnp.where(sel, b, hi)
-    wpk[0] = lo
-    wpk[1] = hi
+        return lo, hi
+
+    own_p.wait()
+    pk[0], pk[1] = pack([pr[H + i, H : H + ny, 0:nz] for i in range(nx)], ZS)
 
     n_peers = 3 * group - 1
     n_peers = n_peers - jnp.where(mz == 0, group, 0) - jnp.where(mz == gz - 1, group, 0)
     pl.semaphore_wait(barrier, n_peers)
 
-    def span(d, n, h, big):
+    def span(d, n, h, skip=0):
         if d == 0:
-            return pl.ds(0, n), pl.ds(big, n)
+            return 0, 0, n
         if d > 0:
-            return pl.ds(n - h, h), pl.ds(0, h)
-        return pl.ds(0, h), pl.ds(big + n, h)
+            return n - skip - h, -skip - h, h
+        return skip, n + skip, h
 
     offsets = [
-        (dx, dy, dz) for dz in (0, -1, 1) for dx in (0, -1, 1) for dy in (0, -1, 1)
+        (dx, dy, dz) for dz in (0, -1, 1) for dx in (-1, 1, 0) for dy in (-1, 1, 0)
         if (dx, dy, dz) != (0, 0, 0)
         and (gx > 1 or dx == 0) and (gy > 1 or dy == 0) and (gz > 1 or dz == 0)
     ]
@@ -125,73 +125,97 @@
     def key(d):
         return (d[0] + 1) * 9 + (d[1] + 1) * 3 + d[2] + 1
 
-    def pcopy(d):
+    near = [(d, 0) for d in offsets if 0 in d]
+    far = [(d, 1) for d in offsets if d[0] != 0 and (d[2] == 0 or d[1] != 0)]
+
+    def edge(buf, got, d):
+        ys, _, n = span(d[1], ny, H)
+        side = 0 if d[2] < 0 else 1
+        slot = (1 - d[0]) * 3 + 1 - d[1]
+        return buf.at[side, pl.ds(ys, n)], got.at[side, slot, pl.ds(ys, n)]
+
+    def pcopy(d, part):
         dx, dy, dz = d
-        to = (mx + dx, my + dy, mz + dz)
+        k = key(d) + 27 * part
+        if dz == 0:
+            xs, xd, n = span(dx, nx, H - NEAR if part else NEAR, NEAR if part else 0)
+            ys, yd, m = span(dy, ny, H)
+            src = pr.at[pl.ds(H + xs, n), pl.ds(H + ys, m), pl.ds(0, nz)]
+            dst = pr.at[pl.ds(H + xd, n), pl.ds(H + yd, m), pl.ds(0, nz)]
+        else:
+            src, dst = edge(pk, bz, d)
+        return pltpu.make_async_remote_copy(
+            src_ref=src, dst_ref=dst, send_sem=psend.at[k], recv_sem=precv.at[k],
+            device_id=(mx + dx, my + dy, mz + dz), device_id_type=MESH)
+
+    def wcopy(d):
+        dx, dy, dz = d
         k = key(d)
         if dz == 0:
-            xs, xd = span(dx, nx, H, H)
-            ys, yd = span(dy, ny, H, H)
-            src, dst = p_ref.at[xs, ys], pr.at[xd, yd, pl.ds(0, nz)]
+            xs, xd, n = span(dx, nx, HW)
+            ys, yd, m = span(dy, ny, H)
+            src = wr.at[:, pl.ds(HW + xs, n), pl.ds(H + ys, m), pl.ds(0, nz)]
+            dst = wr.at[:, pl.ds(HW + xd, n), pl.ds(H + yd, m), pl.ds(0, nz)]
         else:
-            src = pk.at[0 if dz < 0 else 1]
-            dst = bz.at[0 if dz < 0 else 1, (1 - dx) * 3 + 1 - dy]
-        return pltpu.make_async_remote_copy(
-            src_ref=src, dst_ref=dst, send_sem=psend.at[k], recv_sem=precv.at[k],
-            device_id=to, device_id_type=MESH)
-
-    def wcopy(d):
-        dx, dy, dz = d
-        to = (mx + dx, my + dy, mz + dz)
-        k = key(d)
-        if dz == 0:
-            xs, xd = span(dx, nx, HW, HW)
-            ys, yd = span(dy, ny, H, H)
-            src, dst = w_ref.at[:, xs, ys], wr.at[:, xd, yd, pl.ds(0, nz)]
-        else:
-            src = wpk.at[0 if dz < 0 else 1]
-            dst = wzr.at[0 if dz < 0 else 1, (1 - dx) * 3 + 1 - dy]
+            src, dst = edge(wpk, wzr, d)
         return pltpu.make_async_remote_copy(
             src_ref=src, dst_ref=dst, send_sem=wsend.at[k], recv_sem=wrecv.at[k],
-            device_id=to, device_id_type=MESH)
+            device_id=(mx + dx, my + dy, mz + dz), device_id_type=MESH)
 
     def opposite(d):
         return (-d[0], -d[1], -d[2])
 
-    for d in offsets:
-        pl.when(exists(*d))(lambda d=d: pcopy(d).start())
-    for d in offsets:
-        pl.when(exists(*d))(lambda d=d: wcopy(d).start())
-
-    pr[H : H + nx, H : H + ny, 0:nz] = p_ref[...]
-    wr[:, HW : HW + nx, H : H + ny, 0:nz] = w_ref[...]
-
-    for d in offsets:
-        pl.when(exists(*opposite(d)))(lambda d=d: pcopy(d).wait_recv())
-
-    lane_h = lax.broadcasted_iota(jnp.int32, (ny + 2 * H, nz), 1)
-
-    def rows_of(buf, side, ix, comp=None):
+    for d, part in near:
+        pl.when(exists(*d))(lambda d=d, part=part: pcopy(d, part).start())
+
+    for d, part in near:
+        pl.when(exists(*opposite(d)))(lambda d=d, part=part: pcopy(d, part).wait_recv())
+
+    def rows_of(buf, side, ix):
         parts = []
         for iy, (s, n) in enumerate(((ny - H, H), (0, ny), (0, H))):
             parts.append(buf[side, ix * 3 + iy, pl.ds(s, n), :])
         return jnp.concatenate(parts, axis=0)
 
-    def clean(buf_lo, buf_hi, at, width):
+    def unpack(buf_lo, buf_hi, at, width):
+        lanes = lax.broadcasted_iota(jnp.int32, buf_lo.shape, 1)
         right = buf_lo if at == 0 else pltpu.roll(buf_lo, nz - at, 1)
         left = pltpu.roll(buf_hi, (2 * nz - width - at) % nz, 1)
-        return jnp.where(lane_h < width, right, jnp.where(lane_h >= nz - width, left, 0.0))
+        return jnp.where(lanes < width, right, jnp.where(lanes >= nz - width, left, 0.0))
 
     okmask = m2[...] > 0.5
-    for ix, (first, low, n) in enumerate(((nx - H, 0, H), (0, H, nx), (0, H + nx, H))):
-        right, left = rows_of(bz, 0, ix), rows_of(bz, 1, ix)
-        for i in range(n):
+
+    def plane_ok(p):
+        x = mx * nx + p - H
+        return okmask & ((x >= 0) & (x < gx * nx))
+
+    right, left = rows_of(bz, 0, 1), rows_of(bz, 1, 1)
+    for i in range(nx):
+        p = H + i
+        halo = unpack(right, left, ZS * i, ZS)
+        pr[p, :, nz:] = jnp.where(okmask[:, nz:], halo, 0.0)
+        for rows in (slice(0, H), slice(H + ny, 2 * H + ny)):
+            pr[p, rows, 0:nz] = jnp.where(okmask[rows, :nz], pr[p, rows, 0:nz], 0.0)
+    none = jnp.zeros((H, nz), jnp.float32)
+    for ix, first, low in ((0, nx - NEAR, H - NEAR), (2, 0, H + nx)):
+        right, left = bz[0, ix * 3 + 1], bz[1, ix * 3 + 1]
+        for i in range(NEAR):
             p = low + i
-            halo = clean(right, left, ZS * (first + i), ZS)
-            x = mx * nx + p - H
-            good = okmask & ((x >= 0) & (x < gx * nx))
+            halo = unpack(right, left, ZS * (first + i), ZS)
+            halo = jnp.concatenate([none, halo, none], axis=0)
+            good = plane_ok(p)
             pr[p, :, 0:nz] = jnp.where(good[:, :nz], pr[p, :, 0:nz], 0.0)
             pr[p, :, nz:] = jnp.where(good[:, nz:], halo, 0.0)
+
+    def far_planes():
+        for ix, first, low in ((0, nx - H, 0), (2, 0, H + nx)):
+            right, left = rows_of(bz, 0, ix), rows_of(bz, 1, ix)
+            for i in range(H):
+                p = low + i
+                halo = unpack(right, left, ZS * (first + i), ZS)
+                good = plane_ok(p)
+                pr[p, :, 0:nz] = jnp.where(good[:, :nz], pr[p, :, 0:nz], 0.0)
+                pr[p, :, nz:] = jnp.where(good[:, nz:], halo, 0.0)
 
     ry, rz = ny + 2 * H, 2 * nz
 
@@ -413,10 +437,22 @@
 
         loop(low, high, at)
 
-    pre(pr, va, 1, nx + 2 * H - 1)
+    pre(pr, va, H - 1, H + nx + 1)
     coarse_source(0, pr, va)
+    for d, part in far:
+        pl.when(exists(*d))(lambda d=d, part=part: pcopy(d, part).start())
+    own_w.wait()
+    wpk[0], wpk[1] = pack(
+        [wr[e, HW + i, H : H + ny, 0:nz] for e in range(3) for i in range(nx)], HW)
+    for d in offsets:
+        pl.when(exists(*d))(lambda d=d: wcopy(d).start())
     coarse_gather(0)
     coarse(0)
+    for d, part in far:
+        pl.when(exists(*opposite(d)))(lambda d=d, part=part: pcopy(d, part).wait_recv())
+    far_planes()
+    pre(pr, va, 1, H + 1)
+    pre(pr, va, H + nx - 1, nx + 2 * H - 1)
     correct(va, 1, nx + 2 * H - 1)
     post(pr, va, vb, 2, nx + 2 * H - 2)
     post(pr, vb, va, 3, nx + 2 * H - 3)
@@ -436,15 +472,10 @@
         right, left = rows_of(wzr, 0, ix), rows_of(wzr, 1, ix)
         for e in range(3):
             for i in range(n):
-                p = low + i
-                halo = clean(right, left, HW * (e * nx + first + i), HW)
-                x = mx * nx + p - HW
-                good = okmask & ((x >= 0) & (x < gx * nx))
-                wr[e, p, :, 0:nz] = jnp.where(good[:, :nz], wr[e, p, :, 0:nz], 0.0)
-                wr[e, p, :, nz:] = jnp.where(good[:, nz:], halo, 0.0)
+                wr[e, low + i, :, nz:] = unpack(right, left, HW * (e * nx + first + i), HW)
 
     def momentum(p):
-        m = sx(p) * m2[...]
+        m = sx(p) * m2[...] > 0.5
         q = p - (H - HW)
         w0, w1, w2 = 0.5 * wr[0, q], 0.5 * wr[1, q], 0.5 * wr[2, q]
         for d in range(3):
@@ -452,9 +483,11 @@
             yu, yd, zu, zd = up(c, 0), down(c, 0), up(c, 1), down(c, 1)
             total = ((n + s) + (yu + yd)) + (zu + zd)
             conv = w0 * (n - s) + w1 * (yu - yd) + w2 * (zu - zd)
-            flux[d, p] = (7.0 * c - total + conv) * m
+            flux[d, p] = jnp.where(m, 7.0 * c - total + conv, 0.0)
 
     loop(H - HW, H + nx + HW, momentum, 1)
+    for d, part in near + far:
+        pl.when(exists(*d))(lambda d=d, part=part: pcopy(d, part).wait_send())
 
     def product(p):
         f1, f2 = flux[1, p], flux[2, p]
@@ -532,7 +565,6 @@
     for d in offsets:
         @pl.when(exists(*d))
         def _(d=d):
-            pcopy(d).wait_send()
             wcopy(d).wait_send()
     peers(lambda t, ax, ay, dz: gcopy(0, t, ax, ay, dz, me).wait_send())
     peers(lambda t, ax, ay, dz: gcopy(1, t, ax, ay, dz, me).wait_send())
@@ -560,12 +592,12 @@
         V(2, cx // 2, cy, nz), V(2, 2, cy, nz),
         V(2, group, cx // 2, cy, nz), V(2, group, 2, cy, nz),
         V(6, ny, nz), V(6, ny, nz),
-        D(27), D(27), D(27), D(27), D(2, group, 3), D(2, group, 3), D(6), D(6),
+        D(2), D(54), D(54), D(27), D(27), D(2, group, 3), D(2, group, 3), D(6), D(6),
     ]
     return pl.pallas_call(
         functools.partial(kernel, counts, (nx, ny, nz)),
         out_shape=jax.ShapeDtypeStruct(pressure.shape, jnp.float32),
-        in_specs=[pl.BlockSpec(memory_space=pltpu.VMEM)] * 2,
+        in_specs=[pl.BlockSpec(memory_space=pl.ANY)] * 2,
         out_specs=pl.BlockSpec(memory_space=pltpu.VMEM),
         scratch_shapes=scratch,
         compiler_params=pltpu.CompilerParams(collective_id=0, has_side_effects=True),

time: 45 us -> 36.9 us (0.82)
  Pallas kernels: 43.3 us -> 35.2 us
    pallas_call x1, Pallas kernels: 43.3 us -> 35.2 us  [body(): pl.pallas_call(functools.partial(kernel, counts, (nx, ny, nz)), out_shape...]
where the time goes in v2:
time: 36.9 us; the launch traced here: 36.8 us
  Pallas kernels  35.2 us (95%)
  local copies, waits for them, and re-layouts  1.54 us (4%)
    pallas_call x1, Pallas kernels, body(): pl.pallas_call(functools.partial(kernel, counts, (nx, ny, nz)), out_shape...  35.2 us
    unnamed x1, local copies, waits for them, and re-layouts  1.54 us

profile of v2, /device:TPU:0, one launch (start us, length us, event | category | flops | bytes accessed | tf_op | source)
XLA Modules:
  0.0 36.8 jit_solution(3143526740259318883)
XLA Ops:
  0.0 35.2 %shard_map.28 = f32[12,16,128]{2,1,0:T(8,128)} custom-call(f32[12,16,128]{2,1,0:T(8,128)} %p_ref.1, f32[3,12,16,128]{3,2,1,0:T(8,128)} %w_ref.1), custom_call_target="tpu_custom_call" | custom-call | tf_op jit(solution)/shard_map/pallas_call | solution.py:597
  35.2 1.5 %copy.4 = f32[12,16,128]{2,1,0:T(8,128)} copy(f32[12,16,128]{2,1,0:T(8,128)} %shard_map.28) | data formatting | bytes 196608

commit v3 on v2

--- a/solution.py
+++ b/solution.py
@@ -14,8 +14,9 @@
 H = 8
 HW = 3
 ZS = 8
+DEEP = 14
 L1S = 16
-UNROLL = 6
+UNROLL = 12
 NEAR = 2
 
 
@@ -59,6 +60,9 @@
 
     barrier = pltpu.get_barrier_semaphore()
 
+    def reached(ax, ay):
+        return (abs(ax - mx) <= -(-DEEP // cx)) & (abs(ay - my) <= -(-DEEP // cy))
+
     def peers(act):
         def at(t):
             ax, ay = t // gy, t % gy
@@ -67,7 +71,7 @@
                 if dz == 0:
                     ok = t != me
 
-                @pl.when(ok)
+                @pl.when(ok & reached(ax, ay))
                 def _():
                     act(t, ax, ay, dz)
 
@@ -105,8 +109,11 @@
     own_p.wait()
     pk[0], pk[1] = pack([pr[H + i, H : H + ny, 0:nz] for i in range(nx)], ZS)
 
-    n_peers = 3 * group - 1
-    n_peers = n_peers - jnp.where(mz == 0, group, 0) - jnp.where(mz == gz - 1, group, 0)
+    rx, ry = -(-DEEP // cx), -(-DEEP // cy)
+    wide = jnp.minimum(mx + rx, gx - 1) - jnp.maximum(mx - rx, 0) + 1
+    tall_ = jnp.minimum(my + ry, gy - 1) - jnp.maximum(my - ry, 0) + 1
+    deep = jnp.minimum(mz + 1, gz - 1) - jnp.maximum(mz - 1, 0) + 1
+    n_peers = wide * tall_ * deep - 1
     pl.semaphore_wait(barrier, n_peers)
 
     def span(d, n, h, skip=0):
@@ -334,7 +341,7 @@
                 if dz == 0:
                     ok = t != me
 
-                @pl.when(ok)
+                @pl.when(ok & reached(ax, ay))
                 def _():
                     gcopy(turn, t, ax, ay, dz, t).wait_recv()
 
@@ -348,7 +355,7 @@
                 right = pltpu.roll(m2r[turn, t, 0], (cz - L1S * i) % nz, 1)
                 left = pltpu.roll(m2r[turn, t, 1], (2 * nz - L1S - L1S * i) % nz, 1)
                 whole = jnp.where(lane8 < cz, body, jnp.where(lane8 < nz - L1S, right, left))
-                b1[1 + ax * cx + i, 4 + cy * ay : 4 + cy * (ay + 1)] = jnp.where(zin1, whole, 0.0)
+                b1[1 + ax * cx + i, 4 + cy * ay : 4 + cy * (ay + 1)] = jnp.where(zin1 & reached(ax, ay), whole, 0.0)
 
     def coarse(turn):
         cb1 = OMEGA / (6.0 * 0.25)
@@ -485,7 +492,7 @@
             conv = w0 * (n - s) + w1 * (yu - yd) + w2 * (zu - zd)
             flux[d, p] = jnp.where(m, 7.0 * c - total + conv, 0.0)
 
-    loop(H - HW, H + nx + HW, momentum, 1)
+    loop(H - HW, H + nx + HW, momentum, 3)
     for d, part in near + far:
         pl.when(exists(*d))(lambda d=d, part=part: pcopy(d, part).wait_send())
 

time: 36.9 us -> 35.5 us (0.962)
  Pallas kernels: 35.2 us -> 33.8 us
    pallas_call x1, Pallas kernels: 35.2 us -> 33.8 us  [body(): pl.pallas_call(functools.partial(kernel, counts, (nx, ny, nz)), out_shape...]
where the time goes in v3:
time: 35.5 us; the launch traced here: 35.4 us
  Pallas kernels  33.8 us (95%)
  local copies, waits for them, and re-layouts  1.54 us (4%)
    pallas_call x1, Pallas kernels, body(): pl.pallas_call(functools.partial(kernel, counts, (nx, ny, nz)), out_shape...  33.8 us
    unnamed x1, local copies, waits for them, and re-layouts  1.54 us

profile of v3, /device:TPU:0, one launch (start us, length us, event | category | flops | bytes accessed | tf_op | source)
XLA Modules:
  0.0 35.4 jit_solution(7687943980034490716)
XLA Ops:
  0.0 33.8 %shard_map.28 = f32[12,16,128]{2,1,0:T(8,128)} custom-call(f32[12,16,128]{2,1,0:T(8,128)} %p_ref.1, f32[3,12,16,128]{3,2,1,0:T(8,128)} %w_ref.1), custom_call_target="tpu_custom_call" | custom-call | tf_op jit(solution)/shard_map/pallas_call | solution.py:604
  33.8 1.5 %copy.4 = f32[12,16,128]{2,1,0:T(8,128)} copy(f32[12,16,128]{2,1,0:T(8,128)} %shard_map.28) | data formatting | bytes 196608
